TPU v7x, 32 devices: a whole 2x2x4 slice. The times are simulated.
32 devices in a mesh: slab: 8 (over y, x, core), det: 4 (over z).
Axes of the slice: x: 2, y: 2, z: 4, core: 2. Of those that a mesh axis runs over, the one named last changes fastest.
Arguments:
- traces: float32 [32, 128, 4096], P(('slab', 'det')), may hold values from -6 to 6
- tables: bfloat16 [32, 256, 2048], P('slab', None, 'det'), may hold values from -0.0625 to 0.0625
- slab_range: int32 [32, 2], P(('slab', 'det')), may hold values from 0 to 7, as said below
- table_slot: int32 [32, 7], P(('slab', 'det')), may hold values from 0 to 3
- sample_start: int32 [32, 7], P(('slab', 'det')), may hold values from 0 to 3840
Outputs:
- image: float32 [128, 16384], P(None, ('slab', 'det'))
Inputs may be any that keep to these rules, and one draw needn't show every extreme that they name: For detector d with home slab g = d // 4: max(0, g - 3) <= slab_range[d, 0] <= g <= slab_range[d, 1] <= min(7, g + 3); some detectors reach the full 3 on both sides where the grid allows.
All inputs are finite; a program needn't handle non-finite values.
Results may differ from a plain program's by a relative error of at most 0.007.
Values may be sent and summed in bfloat16 or wider, within the bound.
A program may use at most 64 MiB of HBM per device.

v0:
```python
import jax
import jax.numpy as jnp
from jax import lax
from jax.sharding import PartitionSpec as P

KWIN = 256
NTAB = 4
RANGE = 3


def shifted(x, axis, by):
    peers = lax.axis_size(axis)
    pairs = [(i, i + by) for i in range(peers) if 0 <= i + by < peers]
    return lax.ppermute(x, axis, pairs)


def cut_windows(trace_rows, starts):

    def single(trace_row, first_index):
        return lax.dynamic_slice_in_dim(trace_row, first_index, KWIN, 1)

    return jax.vmap(single)(trace_rows, starts)


def bin_windows(windows, slot_ids, active):
    onehot = (slot_ids[:, None] == jnp.arange(NTAB, dtype=jnp.int32)[None, :]) & active[:, None]
    onehot = onehot.astype(jnp.bfloat16)
    return jnp.einsum("it,ifk->tfk", onehot, windows, preferred_element_type=jnp.float32)


def body(traces, tables, slab_range, table_slot, sample_start):
    position = lax.axis_index("slab")
    samples = traces.astype(jnp.bfloat16)
    own_active = (slab_range[:, 0] <= position) & (position <= slab_range[:, 1])
    stacked = bin_windows(
        cut_windows(samples, sample_start[:, RANGE]), table_slot[:, RANGE], own_active
    )
    for offset in list(range(-RANGE, 0)) + list(range(1, RANGE + 1)):
        target = position + offset
        active = (slab_range[:, 0] <= target) & (target <= slab_range[:, 1])
        windows = cut_windows(samples, sample_start[:, offset + RANGE])
        windows = windows * active[:, None, None].astype(jnp.bfloat16)
        arrived_windows, arrived_slots = shifted(
            (windows, table_slot[:, offset + RANGE]), "slab", offset
        )
        everything = jnp.ones(arrived_slots.shape, jnp.bool_)
        stacked = stacked + bin_windows(arrived_windows, arrived_slots, everything)
    binned = stacked.astype(jnp.bfloat16)
    partial_image = jnp.einsum(
        "tfk,tkv->fv",
        binned,
        lax.all_gather(tables, "det", axis=2, tiled=True),
        preferred_element_type=jnp.float32,
    )
    return lax.psum_scatter(partial_image, "det", scatter_dimension=1, tiled=True)


def solution(mesh):
    placed = (
        P(("slab", "det"), None, None),
        P("slab", None, "det"),
        P(("slab", "det"), None),
        P(("slab", "det"), None),
        P(("slab", "det"), None),
    )
    return jax.shard_map(
        body, mesh=mesh, in_specs=placed, out_specs=P(None, ("slab", "det")), check_vma=False
    )
```

profile of v0, /device:TPU:0, one launch (start us, length us, event | category | flops | bytes accessed | tf_op | source)
XLA Modules:
  0.0 129.3 jit_solution(1520195266104620349)
XLA Ops:
  6.5 0.7 all-gather.2.cloned.1.call-update
  7.3 1.6 %fusion.21 = (s32[1,1]{1,0:T(1,128)}, s32[1,1]{1,0:T(1,128)}, s32[1,1]{1,0:T(1,128)}, s32[1,1]{1,0:T(1,128)}, s32[1,1]{1,0:T(1,128)}, /*index=5*/s32[1,1]{1,0:T(1,128)}, s32[1,1]{1,0:T(1,128)}) fusion(s32[1,7]{1,0:T(1,128)} %param.8), kind=kLoop, calls=%fused_computation.43 | loop fusion | bytes 56 | tf_op jit(solution)/shard_map/slice | solution.py:36
  8.9 3.0 %collective-permute-start.6 = (s32[1]{0:T(128)}, s32[1]{0:T(128)}, u32[]{:S(2)}, u32[]{:S(2)}) collective-permute-start(s32[1]{0:T(128)} %bitcast.33), channel_id=1, source_target_pairs={{0,4},{4,8},{8,12},{12,16},{16,20},{20,24},{24,28},{1,5},{5,9},{9,... | collective-permute-start | bytes 20 | tf_op jit(solution)/shard_map/ppermute | solution.py:14
  11.9 1.3 collective-permute-start.4
  13.1 1.3 collective-permute-start.2
  14.4 1.3 collective-permute-start
  15.7 7.7 %collective-permute-start.10 = (s32[1]{0:T(128)}, s32[1]{0:T(128)}, u32[]{:S(2)}, u32[]{:S(2)}) collective-permute-start(s32[1]{0:T(128)} %bitcast.49), channel_id=1, source_target_pairs={{0,12},{4,16},{8,20},{12,24},{16,28},{1,13},{5,17},{9,21},{13,25},... | collective-permute-start | bytes 20 | tf_op jit(solution)/shard_map/ppermute | solution.py:14
  23.4 1.3 %fusion.23 = (s32[1,1]{1,0:T(1,128)}, s32[1,1]{1,0:T(1,128)}) fusion(s32[1,2]{1,0:T(1,128)} %param.7), kind=kLoop, calls=%fused_computation.45 | loop fusion | bytes 16 | tf_op jit(solution)/shard_map/slice | solution.py:34
  33.7 1.6 %fusion.22 = (s32[1,1]{1,0:T(1,128)}, s32[1,1]{1,0:T(1,128)}, s32[1,1]{1,0:T(1,128)}, s32[1,1]{1,0:T(1,128)}, s32[1,1]{1,0:T(1,128)}, /*index=5*/s32[1,1]{1,0:T(1,128)}, s32[1,1]{1,0:T(1,128)}) fusion(s32[1,7]{1,0:T(1,128)} %param.9), kind=kLoop, calls=%fused_computation.44 | loop fusion | bytes 56 | tf_op jit(solution)/shard_map/slice | solution.py:36
  44.2 1.7 %convert_element_type.10 = bf16[1,128,4096]{2,1,0:T(8,128)(2,1)S(1)} convert(f32[1,128,4096]{2,1,0:T(8,128)} %param.5) | non-fusion elementwise | flops 524288 | bytes 3145728 | tf_op jit(solution)/shard_map/convert_element_type | solution.py:33
  51.2 5.9 %collective-permute-start.8 = (s32[1]{0:T(128)}, s32[1]{0:T(128)}, u32[]{:S(2)}, u32[]{:S(2)}) collective-permute-start(s32[1]{0:T(128)} %bitcast.41), channel_id=1, source_target_pairs={{0,8},{4,12},{8,16},{12,20},{16,24},{20,28},{1,9},{5,13},{9,17},{1... | collective-permute-start | bytes 20 | tf_op jit(solution)/shard_map/ppermute | solution.py:14
  57.1 0.7 fusion.18
  57.8 1.3 %collective-permute-start.11 = (bf16[1,128,256]{2,1,0:T(8,128)(2,1)S(1)}, bf16[1,128,256]{2,1,0:T(8,128)(2,1)S(1)}, u32[]{:S(2)}, u32[]{:S(2)}) collective-permute-start(bf16[1,128,256]{2,1,0:T(8,128)(2,1)S(1)} %get-tuple-element.83), channel_id=1, source_target_pairs={{0,12},{4,16},{8,20},{12,24},{16,28},{1,13},{5,17},{9,21},{13,25},... | collective-permute-start | bytes 196616 | tf_op jit(solution)/shard_map/ppermute | solution.py:14
  59.8 2.9 %collective-permute-start.9 = (bf16[1,128,256]{2,1,0:T(8,128)(2,1)S(1)}, bf16[1,128,256]{2,1,0:T(8,128)(2,1)S(1)}, u32[]{:S(2)}, u32[]{:S(2)}) collective-permute-start(bf16[1,128,256]{2,1,0:T(8,128)(2,1)S(1)} %get-tuple-element.84), channel_id=1, source_target_pairs={{0,8},{4,12},{8,16},{12,20},{16,24},{20,28},{1,9},{5,13},{9,17},{1... | collective-permute-start | bytes 196616 | tf_op jit(solution)/shard_map/ppermute | solution.py:14
  63.3 1.3 %collective-permute-start.7 = (bf16[1,128,256]{2,1,0:T(8,128)(2,1)S(1)}, bf16[1,128,256]{2,1,0:T(8,128)(2,1)S(1)}, u32[]{:S(2)}, u32[]{:S(2)}) collective-permute-start(bf16[1,128,256]{2,1,0:T(8,128)(2,1)S(1)} %get-tuple-element.85), channel_id=1, source_target_pairs={{0,4},{4,8},{8,12},{12,16},{16,20},{20,24},{24,28},{1,5},{5,9},{9,... | collective-permute-start | bytes 196616 | tf_op jit(solution)/shard_map/ppermute | solution.py:14
  65.2 1.3 collective-permute-start.5
  67.2 1.3 collective-permute-start.3
  68.5 0.7 fusion.19
  69.2 1.3 collective-permute-start.1
  70.6 4.5 %collective-permute-done.3 = bf16[1,128,256]{2,1,0:T(8,128)(2,1)S(1)} collective-permute-done((bf16[1,128,256]{2,1,0:T(8,128)(2,1)S(1)}, bf16[1,128,256]{2,1,0:T(8,128)(2,1)S(1)}, u32[]{:S(2)}, u32[]{:S(2)}) %collective-permute-start.3) | collective-permute-done | bytes 65568 | tf_op jit(solution)/shard_map/ppermute | solution.py:14
  75.1 1.9 %collective-permute-done.1 = bf16[1,128,256]{2,1,0:T(8,128)(2,1)S(1)} collective-permute-done((bf16[1,128,256]{2,1,0:T(8,128)(2,1)S(1)}, bf16[1,128,256]{2,1,0:T(8,128)(2,1)S(1)}, u32[]{:S(2)}, u32[]{:S(2)}) %collective-permute-start.1) | collective-permute-done | bytes 65568 | tf_op jit(solution)/shard_map/ppermute | solution.py:14
  77.0 15.4 %all-gather.2.cloned.1.call-done = bf16[4,256,2048]{2,1,0:T(8,128)(2,1)} async-done(((bf16[4,256,512]{2,1,0:T(8,128)(2,1)}), bf16[4,256,2048]{2,1,0:T(8,128)(2,1)}) %all-gather.2.cloned.1.call-update) | async-done | bytes 4194320 | tf_op jit(solution)/shard_map/all_gather | solution.py:52
  92.4 4.1 %convolution_bitcast_fusion = f32[128,2048]{1,0:T(8,128)} fusion(bf16[4,256,2048]{2,1,0:T(8,128)(2,1)} %all-gather.2.cloned.1.call-done, f32[128,256]{1,0:T(8,128)S(1)} %bitcast_convert_fusion, f32[4]{0:T(128)S(1)} %fusion.20, f32[128,256]{1,0:T(8,128)S(1)} %bitcast_convert_fusion.1, f32[4]{0:T(128)S(1)} %fusion.19, f32[128,256]{1,0:T(8,128)S(1)} %bitcast_convert_fusion.2, ...), kind=kOutput, calls=%fused_computation | convolution fusion | flops 538705920 | bytes 6160496 | tf_op jit(solution)/shard_map/tfk,tkv->fv/dot_general | solution.py:49
  96.5 25.9 %reduce-scatter.2.cloned.1.call-done = f32[128,512]{1,0:T(8,128)} async-done(((f32[128,2048]{1,0:T(8,128)}), f32[128,512]{1,0:T(8,128)}) %reduce-scatter.2.cloned.1.call-update) | async-done | bytes 262160 | tf_op jit(solution)/shard_map/reduce_scatter | solution.py:55
  (25 shorter events, 3.5 us)
Async XLA Ops:
  6.5 85.9 %all-gather.2.cloned.1.call-start = ((), (), s32[]{:S(2)}) async-start(), calls=%async_computation.1 | async-start | bytes 5242880 | tf_op jit(solution)/shard_map/all_gather | solution.py:52
  7.3 115.2 %reduce-scatter.2.cloned.1.call-start = ((), (), s32[]{:S(2)}) async-start(), calls=%async_computation.2 | async-start | bytes 1310720 | tf_op jit(solution)/shard_map/reduce_scatter | solution.py:55
  8.9 42.3 %collective-permute-start.6 = (s32[1]{0:T(128)}, s32[1]{0:T(128)}, u32[]{:S(2)}, u32[]{:S(2)}) collective-permute-start(s32[1]{0:T(128)} %bitcast.33), channel_id=1, source_target_pairs={{0,4},{4,8},{8,12},{12,16},{16,20},{20,24},{24,28},{1,5},{5,9},{9,... | collective-permute-start | bytes 20 | tf_op jit(solution)/shard_map/ppermute | solution.py:14
  11.9 46.0 %collective-permute-start.4 = (s32[1]{0:T(128)}, s32[1]{0:T(128)}, u32[]{:S(2)}, u32[]{:S(2)}) collective-permute-start(s32[1]{0:T(128)} %bitcast.25), channel_id=1, source_target_pairs={{4,0},{8,4},{12,8},{16,12},{20,16},{24,20},{28,24},{5,1},{9,5},{13... | collective-permute-start | bytes 20 | tf_op jit(solution)/shard_map/ppermute | solution.py:14
  13.1 46.6 %collective-permute-start.2 = (s32[1]{0:T(128)}, s32[1]{0:T(128)}, u32[]{:S(2)}, u32[]{:S(2)}) collective-permute-start(s32[1]{0:T(128)} %bitcast.17), channel_id=1, source_target_pairs={{8,0},{12,4},{16,8},{20,12},{24,16},{28,20},{9,1},{13,5},{17,9},{2... | collective-permute-start | bytes 20 | tf_op jit(solution)/shard_map/ppermute | solution.py:14
  14.4 48.8 %collective-permute-start = (s32[1]{0:T(128)}, s32[1]{0:T(128)}, u32[]{:S(2)}, u32[]{:S(2)}) collective-permute-start(s32[1]{0:T(128)} %bitcast.9), channel_id=1, source_target_pairs={{12,0},{16,4},{20,8},{24,12},{28,16},{13,1},{17,5},{21,9},{25,13},... | collective-permute-start | bytes 20 | tf_op jit(solution)/shard_map/ppermute | solution.py:14
  15.7 49.5 %collective-permute-start.10 = (s32[1]{0:T(128)}, s32[1]{0:T(128)}, u32[]{:S(2)}, u32[]{:S(2)}) collective-permute-start(s32[1]{0:T(128)} %bitcast.49), channel_id=1, source_target_pairs={{0,12},{4,16},{8,20},{12,24},{16,28},{1,13},{5,17},{9,21},{13,25},... | collective-permute-start | bytes 20 | tf_op jit(solution)/shard_map/ppermute | solution.py:14
  51.2 16.0 %collective-permute-start.8 = (s32[1]{0:T(128)}, s32[1]{0:T(128)}, u32[]{:S(2)}, u32[]{:S(2)}) collective-permute-start(s32[1]{0:T(128)} %bitcast.41), channel_id=1, source_target_pairs={{0,8},{4,12},{8,16},{12,20},{16,24},{20,28},{1,9},{5,13},{9,17},{1... | collective-permute-start | bytes 20 | tf_op jit(solution)/shard_map/ppermute | solution.py:14
  57.8 11.4 %collective-permute-start.11 = (bf16[1,128,256]{2,1,0:T(8,128)(2,1)S(1)}, bf16[1,128,256]{2,1,0:T(8,128)(2,1)S(1)}, u32[]{:S(2)}, u32[]{:S(2)}) collective-permute-start(bf16[1,128,256]{2,1,0:T(8,128)(2,1)S(1)} %get-tuple-element.83), channel_id=1, source_target_pairs={{0,12},{4,16},{8,20},{12,24},{16,28},{1,13},{5,17},{9,21},{13,25},... | collective-permute-start | bytes 196616 | tf_op jit(solution)/shard_map/ppermute | solution.py:14
  59.8 10.7 %collective-permute-start.9 = (bf16[1,128,256]{2,1,0:T(8,128)(2,1)S(1)}, bf16[1,128,256]{2,1,0:T(8,128)(2,1)S(1)}, u32[]{:S(2)}, u32[]{:S(2)}) collective-permute-start(bf16[1,128,256]{2,1,0:T(8,128)(2,1)S(1)} %get-tuple-element.84), channel_id=1, source_target_pairs={{0,8},{4,12},{8,16},{12,20},{16,24},{20,28},{1,9},{5,13},{9,17},{1... | collective-permute-start | bytes 196616 | tf_op jit(solution)/shard_map/ppermute | solution.py:14
  63.3 7.2 %collective-permute-start.7 = (bf16[1,128,256]{2,1,0:T(8,128)(2,1)S(1)}, bf16[1,128,256]{2,1,0:T(8,128)(2,1)S(1)}, u32[]{:S(2)}, u32[]{:S(2)}) collective-permute-start(bf16[1,128,256]{2,1,0:T(8,128)(2,1)S(1)} %get-tuple-element.85), channel_id=1, source_target_pairs={{0,4},{4,8},{8,12},{12,16},{16,20},{20,24},{24,28},{1,5},{5,9},{9,... | collective-permute-start | bytes 196616 | tf_op jit(solution)/shard_map/ppermute | solution.py:14
  65.2 5.3 %collective-permute-start.5 = (bf16[1,128,256]{2,1,0:T(8,128)(2,1)S(1)}, bf16[1,128,256]{2,1,0:T(8,128)(2,1)S(1)}, u32[]{:S(2)}, u32[]{:S(2)}) collective-permute-start(bf16[1,128,256]{2,1,0:T(8,128)(2,1)S(1)} %get-tuple-element.86), channel_id=1, source_target_pairs={{4,0},{8,4},{12,8},{16,12},{20,16},{24,20},{28,24},{5,1},{9,5},{13... | collective-permute-start | bytes 196616 | tf_op jit(solution)/shard_map/ppermute | solution.py:14
  67.2 7.9 %collective-permute-start.3 = (bf16[1,128,256]{2,1,0:T(8,128)(2,1)S(1)}, bf16[1,128,256]{2,1,0:T(8,128)(2,1)S(1)}, u32[]{:S(2)}, u32[]{:S(2)}) collective-permute-start(bf16[1,128,256]{2,1,0:T(8,128)(2,1)S(1)} %get-tuple-element.87), channel_id=1, source_target_pairs={{8,0},{12,4},{16,8},{20,12},{24,16},{28,20},{9,1},{13,5},{17,9},{2... | collective-permute-start | bytes 196616 | tf_op jit(solution)/shard_map/ppermute | solution.py:14
  69.2 7.8 %collective-permute-start.1 = (bf16[1,128,256]{2,1,0:T(8,128)(2,1)S(1)}, bf16[1,128,256]{2,1,0:T(8,128)(2,1)S(1)}, u32[]{:S(2)}, u32[]{:S(2)}) collective-permute-start(bf16[1,128,256]{2,1,0:T(8,128)(2,1)S(1)} %get-tuple-element.88), channel_id=1, source_target_pairs={{12,0},{16,4},{20,8},{24,12},{28,16},{13,1},{17,5},{21,9},{25,13},... | collective-permute-start | bytes 196616 | tf_op jit(solution)/shard_map/ppermute | solution.py:14
Sparse Core Ops, SparseCore 0:
  8.9 83.4 all-gather.1
  96.6 25.7 reduce-scatter.1
where the time goes:
time: 130 us; the launch traced here: 129 us
  waiting for transfers between devices  48.5 us (37%)
  between operations  36 us (28%)
  starting transfers between devices  29.8 us (23%)
  other arithmetic  6.48 us (5%)
  local copies, waits for them, and re-layouts  4.5 us (3%)
  matrix products  4.07 us (3%)
    ppermute x12, starting transfers between devices, shifted(): return lax.ppermute(x, axis, pairs)  29.7 us
    reduce_scatter x1, waiting for transfers between devices, body(): lax.psum_scatter(partial_image, 'det', scatter_dimension=1, tiled=True)  25.9 us
    all_gather x1, waiting for transfers between devices, body(): lax.all_gather(tables, 'det', axis=2, tiled=True)  15.4 us
    ppermute x12, waiting for transfers between devices, shifted(): return lax.ppermute(x, axis, pairs)  6.42 us
    another operation x14, other arithmetic  4.75 us
    dot_general x1, matrix products, body(): jnp.einsum('tfk,tkv->fv', binned, lax.all_gather(tables, 'det', axis=2, t...  4.07 us
  transfers between devices with their start and end apart: 14, of which 4 were waited for; matrix products, arithmetic and copies ran while one was open for 8% of the time, Pallas kernels for 0%

commit v1 on v0

v1 whole, which is shorter than its diff:
```python
import functools

import jax
import jax.numpy as jnp
from jax import lax
from jax.experimental import pallas as pl
from jax.experimental.pallas import tpu as pltpu
from jax.sharding import PartitionSpec as P

MESH = pl.DeviceIdType.MESH
KWIN = 256
NTAB = 4
RANGE = 3
LANES = 128
OFFSETS = 2 * RANGE + 1


def cut_kernel(n_slab, traces, slab_range, table_slot, sample_start, wins, masks, spans, sems):
    slab = lax.axis_index("slab")
    samp, span = traces.shape[2], spans.shape[2]
    n_quarter, _, rows, _ = wins.shape
    loads, inner = [], []
    for o in range(OFFSETS):
        start = sample_start[0, o]
        tile = jnp.minimum(lax.div(start, LANES), (samp - span) // LANES)
        inner.append(start - tile * LANES)
        first = pl.multiple_of(tile * LANES, LANES)
        loads.append(
            pltpu.make_async_copy(traces.at[0, :, pl.ds(first, span)], spans.at[o], sems.at[o])
        )
        loads[-1].start()
    mask_rows = lax.broadcasted_iota(jnp.int32, masks.shape[1:], 0)
    for o in range(OFFSETS):
        target = slab + (o - RANGE)
        active = (slab_range[0, 0] <= target) & (target <= slab_range[0, 1])
        slot = jnp.where(active, table_slot[0, o], -1)
        masks[o] = (mask_rows == slot).astype(jnp.float32)
    far = lax.broadcasted_iota(jnp.int32, (span, KWIN), 0)
    far = far - lax.broadcasted_iota(jnp.int32, (span, KWIN), 1)
    for o in range(OFFSETS):
        pick = (far == inner[o]).astype(jnp.bfloat16)
        loads[o].wait()
        moved = jnp.dot(spans[o].astype(jnp.bfloat16), pick, preferred_element_type=jnp.float32)
        for q in range(n_quarter):
            wins[q, o] = moved[q * rows : (q + 1) * rows].astype(jnp.bfloat16)


def kernel(
    n_slab, n_det,
    send_win, send_mask, tables, out,
    table_buf, got_win, got_mask,
    part, got_part, total, got_total,
    table_sem, win_send, win_recv, mask_send, mask_recv,
    part_send, part_recv, total_send, total_recv,
):
    slab, det = lax.axis_index("slab"), lax.axis_index("det")
    rows = send_win.shape[2]
    order = sorted(range(1, n_det), key=lambda d: -min(d, n_det - d)) + [0]
    away = [o for o in range(OFFSETS) if o != RANGE]
    away.sort(key=lambda o: -abs(o - RANGE))

    def valid(to):
        return (to >= 0) & (to < n_slab)

    def part_of(d):
        return lax.rem(det + d, n_det)

    table_load = pltpu.make_async_copy(tables, table_buf, table_sem)
    table_load.start()

    barrier = pltpu.get_barrier_semaphore()
    peers = jnp.int32(n_det - 1)
    for o in away:
        peer = slab + (o - RANGE)
        peers = peers + valid(peer).astype(jnp.int32)

        @pl.when(valid(peer))
        def _():
            pl.semaphore_signal(barrier, 1, device_id=(peer, det), device_id_type=MESH)

    for d in order[:-1]:
        pl.semaphore_signal(
            barrier, 1, device_id=(slab, part_of(d)), device_id_type=MESH
        )

    def mask_copy(o):
        return pltpu.make_async_remote_copy(
            src_ref=send_mask.at[o], dst_ref=got_mask.at[o],
            send_sem=mask_send.at[o], recv_sem=mask_recv.at[o],
            device_id=(slab + (o - RANGE), det), device_id_type=MESH,
        )

    def win_copy(c, o):
        return pltpu.make_async_remote_copy(
            src_ref=send_win.at[part_of(order[c]), o], dst_ref=got_win.at[c, o],
            send_sem=win_send.at[c, o], recv_sem=win_recv.at[c, o],
            device_id=(slab + (o - RANGE), det), device_id_type=MESH,
        )

    def part_copy(c):
        d = order[c]
        return pltpu.make_async_remote_copy(
            src_ref=part.at[c], dst_ref=got_part.at[c],
            send_sem=part_send.at[c], recv_sem=part_recv.at[c],
            device_id=(slab, part_of(d)), device_id_type=MESH,
        )

    def total_copy(c):
        d = order[c]
        return pltpu.make_async_remote_copy(
            src_ref=total, dst_ref=got_total.at[c],
            send_sem=total_send.at[c], recv_sem=total_recv.at[c],
            device_id=(slab, part_of(d)), device_id_type=MESH,
        )

    pl.semaphore_wait(barrier, peers)
    for c in range(n_det):
        for o in away:

            @pl.when(valid(slab + (o - RANGE)))
            def _():
                if c == 0:
                    mask_copy(o).start()
                win_copy(c, o).start()

    for o in away:

        @pl.when(jnp.logical_not(valid(slab - (o - RANGE))))
        def _():
            got_mask[o] = jnp.zeros(got_mask.shape[1:], got_mask.dtype)
            for c in range(n_det):
                got_win[c, o] = jnp.zeros(got_win.shape[2:], got_win.dtype)

    for c in range(n_det):
        for o in away:

            @pl.when(valid(slab - (o - RANGE)))
            def _():
                if c == 0:
                    mask_copy(o).wait_recv()
                win_copy(c, o).wait_recv()

        bins = [jnp.zeros((rows, KWIN), jnp.float32) for _ in range(NTAB)]
        for o in range(OFFSETS):
            if o == RANGE:
                win, mask = send_win[part_of(order[c]), o], send_mask
            else:
                win, mask = got_win[c, o], got_mask
            win = win.astype(jnp.float32)
            for t in range(NTAB):
                bins[t] = bins[t] + mask[o, t : t + 1] * win
        for t in range(NTAB):
            part[c, :, t * KWIN : (t + 1) * KWIN] = bins[t].astype(jnp.bfloat16)
        if order[c] != 0:
            part_copy(c).start()

    summed = part[n_det - 1].astype(jnp.float32)
    for c in range(n_det - 1):
        part_copy(c).wait_recv()
        summed = summed + got_part[c].astype(jnp.float32)
    total[...] = summed.astype(jnp.bfloat16)
    for c in range(n_det - 1):
        total_copy(c).start()

    table_load.wait()
    weights = table_buf[...].reshape(NTAB * KWIN, table_buf.shape[2])

    def finish(quarter_sum, d):
        out[pl.ds(pl.multiple_of(part_of(d) * rows, rows), rows), :] = jnp.dot(
            quarter_sum, weights, preferred_element_type=jnp.float32
        )

    finish(total[...], 0)
    nearest = sorted(range(n_det - 1), key=lambda c: min(order[c], n_det - order[c]))
    for c in nearest:
        total_copy(c).wait_recv()
        finish(got_total[c], n_det - order[c])

    for o in away:

        @pl.when(valid(slab + (o - RANGE)))
        def _():
            mask_copy(o).wait_send()
            for c in range(n_det):
                win_copy(c, o).wait_send()

    for c in range(n_det - 1):
        part_copy(c).wait_send()
        total_copy(c).wait_send()


def body(n_slab, n_det, traces, tables, slab_range, table_slot, sample_start):
    _, frames, samp = traces.shape
    voxels = tables.shape[2]
    rows = frames // n_det
    wide = NTAB * KWIN
    mask_rows = -(-NTAB // 8) * 8
    anywhere = pl.BlockSpec(memory_space=pl.ANY)
    scalars = pl.BlockSpec(memory_space=pltpu.SMEM)
    vmem = pl.BlockSpec(memory_space=pltpu.VMEM)
    dma = pltpu.SemaphoreType.DMA
    wins, masks = pl.pallas_call(
        functools.partial(cut_kernel, n_slab),
        out_shape=[
            jax.ShapeDtypeStruct((n_det, OFFSETS, rows, KWIN), jnp.bfloat16),
            jax.ShapeDtypeStruct((OFFSETS, mask_rows, KWIN), jnp.float32),
        ],
        in_specs=[pl.BlockSpec(memory_space=pltpu.HBM), scalars, scalars, scalars],
        out_specs=[vmem, vmem],
        scratch_shapes=[
            pltpu.VMEM((OFFSETS, frames, KWIN + LANES), jnp.float32),
            dma((OFFSETS,)),
        ],
        compiler_params=pltpu.CompilerParams(vmem_limit_bytes=16 * 1024 * 1024),
    )(traces, slab_range, table_slot, sample_start)
    return pl.pallas_call(
        functools.partial(kernel, n_slab, n_det),
        out_shape=jax.ShapeDtypeStruct((frames, voxels), jnp.float32),
        in_specs=[vmem, vmem, anywhere],
        out_specs=vmem,
        scratch_shapes=[
            pltpu.VMEM(tables.shape, jnp.bfloat16),
            pltpu.VMEM((n_det, OFFSETS, rows, KWIN), jnp.bfloat16),
            pltpu.VMEM((OFFSETS, mask_rows, KWIN), jnp.float32),
            pltpu.VMEM((n_det, rows, wide), jnp.bfloat16),
            pltpu.VMEM((n_det, rows, wide), jnp.bfloat16),
            pltpu.VMEM((rows, wide), jnp.bfloat16),
            pltpu.VMEM((n_det, rows, wide), jnp.bfloat16),
            dma,
            dma((n_det, OFFSETS)),
            dma((n_det, OFFSETS)),
            dma((OFFSETS,)),
            dma((OFFSETS,)),
            dma((n_det,)),
            dma((n_det,)),
            dma((n_det,)),
            dma((n_det,)),
        ],
        compiler_params=pltpu.CompilerParams(
            collective_id=0, has_side_effects=True, vmem_limit_bytes=16 * 1024 * 1024
        ),
    )(wins, masks, tables)


def solution(mesh):
    placed = (
        P(("slab", "det"), None, None),
        P("slab", None, "det"),
        P(("slab", "det"), None),
        P(("slab", "det"), None),
        P(("slab", "det"), None),
    )
    return jax.shard_map(
        functools.partial(body, mesh.shape["slab"], mesh.shape["det"]),
        mesh=mesh, in_specs=placed, out_specs=P(None, ("slab", "det")), check_vma=False,
    )
```

time: 130 us -> 32.2 us (0.25)
  waiting for transfers between devices: 48.5 us -> 0 us
  between operations: 36 us -> 0.03 us
  starting transfers between devices: 29.8 us -> 0 us
  Pallas kernels: 0 us -> 27.8 us
  other arithmetic: 6.48 us -> 0 us
  matrix products: 4.07 us -> 0 us
    ppermute x12 -> x0, starting transfers between devices: 29.7 us -> none  [shifted(): return lax.ppermute(x, axis, pairs)]
    pallas_call x0 -> x2, Pallas kernels: none -> 27.8 us  [the longest x1 25.4 us: body(): pl.pallas_call(functools.partial(kernel, n_slab, n_det), out_shape=jax.Sh...]
    reduce_scatter x1 -> x0, waiting for transfers between devices: 25.9 us -> none  [body(): lax.psum_scatter(partial_image, 'det', scatter_dimension=1, tiled=True)]
    all_gather x1 -> x0, waiting for transfers between devices: 15.4 us -> none  [body(): lax.all_gather(tables, 'det', axis=2, tiled=True)]
    ppermute x12 -> x0, waiting for transfers between devices: 6.42 us -> none  [shifted(): return lax.ppermute(x, axis, pairs)]
    another operation x14 -> x0, other arithmetic: 4.75 us -> none
    slice x3 -> x0, local copies, waits for them, and re-layouts: 4.5 us -> none  [the longest x1 1.6 us: body(): sample_start[:, RANGE]]
    unnamed x0 -> x11, local copies, waits for them, and re-layouts: none -> 4.26 us
  transfers between devices with their start and end apart: 14 -> 0, of which waited for: 4 -> 0; matrix products, arithmetic and copies ran while one was open for 8% -> 0% of each run, Pallas kernels for 0% -> 0%
where the time goes in v1:
time: 32.2 us; the launch traced here: 32.1 us
  Pallas kernels  27.8 us (86%)
  local copies, waits for them, and re-layouts  4.26 us (13%)
    pallas_call x1, Pallas kernels, body(): pl.pallas_call(functools.partial(kernel, n_slab, n_det), out_shape=jax.Sh...  25.4 us
    unnamed x11, local copies, waits for them, and re-layouts  4.26 us
    pallas_call x1, Pallas kernels, body(): pl.pallas_call(functools.partial(cut_kernel, n_slab), out_shape=[jax.Shap...  2.33 us

profile of v1, /device:TPU:0, one launch (start us, length us, event | category | flops | bytes accessed | tf_op | source)
XLA Modules:
  0.0 32.1 jit_solution(11882660393598479998)
XLA Ops:
  0.0 0.0 copy-start
  0.0 1.6 %copy-done = f32[1,128,4096]{2,1,0:T(8,128)S(1)} copy-done((f32[1,128,4096]{2,1,0:T(8,128)S(1)}, f32[1,128,4096]{2,1,0:T(8,128)}, u32[]{:S(2)}) %copy-start) | copy-done | bytes 2097176
  1.6 0.0 copy-start.2
  1.6 0.7 %copy-done.2 = s32[1,2]{1,0:T(1,128)S(1)} copy-done((s32[1,2]{1,0:T(1,128)S(1)}, s32[1,2]{1,0:T(1,128)}, u32[]{:S(2)}) %copy-start.2) | copy-done | bytes 32
  2.2 0.0 copy-start.3
  2.2 0.7 %copy-done.3 = s32[1,7]{1,0:T(1,128)S(1)} copy-done((s32[1,7]{1,0:T(1,128)S(1)}, s32[1,7]{1,0:T(1,128)}, u32[]{:S(2)}) %copy-start.3) | copy-done | bytes 52
  2.9 0.0 copy-start.4
  2.9 0.7 %copy-done.4 = s32[1,7]{1,0:T(1,128)S(1)} copy-done((s32[1,7]{1,0:T(1,128)S(1)}, s32[1,7]{1,0:T(1,128)}, u32[]{:S(2)}) %copy-start.4) | copy-done | bytes 52
  3.6 0.0 copy-start.1
  3.6 2.3 %shard_map.55 = (bf16[4,7,32,256]{3,2,1,0:T(8,128)(2,1)S(1)}, f32[7,8,256]{2,1,0:T(8,128)S(1)}) custom-call(f32[1,128,4096]{2,1,0:T(8,128)S(1)} %copy-done, s32[1,2]{1,0:T(1,128)S(1)} %copy-done.2, s32[1,7]{1,0:T(1,128)S(1)} %copy-done.3, s32[1,7]{1,0:T(1,128)S(1)} %copy-done.4), custom_call_target="tpu_custom_call" | custom-call | tf_op jit(solution)/shard_map/pallas_call | solution.py:202
  5.9 0.0 copy-done.1
  5.9 25.4 %shard_map.56 = f32[128,512]{1,0:T(8,128)S(1)} custom-call(bf16[4,7,32,256]{3,2,1,0:T(8,128)(2,1)S(1)} %get-tuple-element.7.send_win, f32[7,8,256]{2,1,0:T(8,128)S(1)} %get-tuple-element.8.send_mask, bf16[4,256,512]{2,1,0:T(8,128)(2,1)S(1)} %copy-done.1), custom_call_target="tpu_custom_call" | custom-call | tf_op jit(solution)/shard_map/pallas_call | solution.py:216
  31.3 0.7 %copy.7 = f32[128,512]{1,0:T(8,128)} copy(f32[128,512]{1,0:T(8,128)S(1)} %shard_map.56) | data formatting | bytes 524288
Async XLA Ops:
  0.0 1.6 %copy-start = (f32[1,128,4096]{2,1,0:T(8,128)S(1)}, f32[1,128,4096]{2,1,0:T(8,128)}, u32[]{:S(2)}) copy-start(f32[1,128,4096]{2,1,0:T(8,128)} %traces.1) | copy-start | bytes 6291460
  1.6 0.7 %copy-start.2 = (s32[1,2]{1,0:T(1,128)S(1)}, s32[1,2]{1,0:T(1,128)}, u32[]{:S(2)}) copy-start(s32[1,2]{1,0:T(1,128)} %slab_range.1) | copy-start | bytes 28
  2.2 0.7 %copy-start.3 = (s32[1,7]{1,0:T(1,128)S(1)}, s32[1,7]{1,0:T(1,128)}, u32[]{:S(2)}) copy-start(s32[1,7]{1,0:T(1,128)} %table_slot.1) | copy-start | bytes 88
  2.9 0.7 %copy-start.4 = (s32[1,7]{1,0:T(1,128)S(1)}, s32[1,7]{1,0:T(1,128)}, u32[]{:S(2)}) copy-start(s32[1,7]{1,0:T(1,128)} %sample_start.1) | copy-start | bytes 88
  3.6 2.3 %copy-start.1 = (bf16[4,256,512]{2,1,0:T(8,128)(2,1)S(1)}, bf16[4,256,512]{2,1,0:T(8,128)(2,1)}, u32[]{:S(2)}) copy-start(bf16[4,256,512]{2,1,0:T(8,128)(2,1)} %tables.1) | copy-start | bytes 3145732

commit v2 on v1

--- a/solution.py
+++ b/solution.py
@@ -15,10 +15,10 @@
 OFFSETS = 2 * RANGE + 1
 
 
-def cut_kernel(n_slab, traces, slab_range, table_slot, sample_start, wins, masks, spans, sems):
+def cut_kernel(n_slab, traces, slab_range, table_slot, sample_start, wins, masks, spans, cuts, mask_buf, sems, out_sems):
     slab = lax.axis_index("slab")
     samp, span = traces.shape[2], spans.shape[2]
-    n_quarter, _, rows, _ = wins.shape
+    _, n_quarter, rows, _ = wins.shape
     loads, inner = [], []
     for o in range(OFFSETS):
         start = sample_start[0, o]
@@ -29,12 +29,14 @@
             pltpu.make_async_copy(traces.at[0, :, pl.ds(first, span)], spans.at[o], sems.at[o])
         )
         loads[-1].start()
-    mask_rows = lax.broadcasted_iota(jnp.int32, masks.shape[1:], 0)
+    mask_rows = lax.broadcasted_iota(jnp.int32, mask_buf.shape[1:], 0)
     for o in range(OFFSETS):
         target = slab + (o - RANGE)
         active = (slab_range[0, 0] <= target) & (target <= slab_range[0, 1])
         slot = jnp.where(active, table_slot[0, o], -1)
-        masks[o] = (mask_rows == slot).astype(jnp.float32)
+        mask_buf[o] = (mask_rows == slot).astype(jnp.float32)
+    stores = [pltpu.make_async_copy(mask_buf, masks, out_sems.at[OFFSETS])]
+    stores[0].start()
     far = lax.broadcasted_iota(jnp.int32, (span, KWIN), 0)
     far = far - lax.broadcasted_iota(jnp.int32, (span, KWIN), 1)
     for o in range(OFFSETS):
@@ -42,15 +44,19 @@
         loads[o].wait()
         moved = jnp.dot(spans[o].astype(jnp.bfloat16), pick, preferred_element_type=jnp.float32)
         for q in range(n_quarter):
-            wins[q, o] = moved[q * rows : (q + 1) * rows].astype(jnp.bfloat16)
+            cuts[o, q] = moved[q * rows : (q + 1) * rows].astype(jnp.bfloat16)
+        stores.append(pltpu.make_async_copy(cuts.at[o], wins.at[o], out_sems.at[o]))
+        stores[-1].start()
+    for store in stores:
+        store.wait()
 
 
 def kernel(
     n_slab, n_det,
-    send_win, send_mask, tables, out,
-    table_buf, got_win, got_mask,
+    wins, masks, tables, out,
+    send_win, send_mask, table_buf, got_win, got_mask,
     part, got_part, total, got_total,
-    table_sem, win_send, win_recv, mask_send, mask_recv,
+    win_load, mask_load, table_sem, win_send, win_recv, mask_send, mask_recv,
     part_send, part_recv, total_send, total_recv,
 ):
     slab, det = lax.axis_index("slab"), lax.axis_index("det")
@@ -65,6 +71,12 @@
     def part_of(d):
         return lax.rem(det + d, n_det)
 
+    loads = [
+        pltpu.make_async_copy(masks, send_mask, mask_load),
+        pltpu.make_async_copy(wins, send_win, win_load),
+    ]
+    for load in loads:
+        load.start()
     table_load = pltpu.make_async_copy(tables, table_buf, table_sem)
     table_load.start()
 
@@ -92,7 +104,7 @@
 
     def win_copy(c, o):
         return pltpu.make_async_remote_copy(
-            src_ref=send_win.at[part_of(order[c]), o], dst_ref=got_win.at[c, o],
+            src_ref=send_win.at[o, part_of(order[c])], dst_ref=got_win.at[c, o],
             send_sem=win_send.at[c, o], recv_sem=win_recv.at[c, o],
             device_id=(slab + (o - RANGE), det), device_id_type=MESH,
         )
@@ -113,6 +125,8 @@
             device_id=(slab, part_of(d)), device_id_type=MESH,
         )
 
+    for load in loads:
+        load.wait()
     pl.semaphore_wait(barrier, peers)
     for c in range(n_det):
         for o in away:
@@ -143,7 +157,7 @@
         bins = [jnp.zeros((rows, KWIN), jnp.float32) for _ in range(NTAB)]
         for o in range(OFFSETS):
             if o == RANGE:
-                win, mask = send_win[part_of(order[c]), o], send_mask
+                win, mask = send_win[o, part_of(order[c])], send_mask
             else:
                 win, mask = got_win[c, o], got_mask
             win = win.astype(jnp.float32)
@@ -202,23 +216,27 @@
     wins, masks = pl.pallas_call(
         functools.partial(cut_kernel, n_slab),
         out_shape=[
-            jax.ShapeDtypeStruct((n_det, OFFSETS, rows, KWIN), jnp.bfloat16),
+            jax.ShapeDtypeStruct((OFFSETS, n_det, rows, KWIN), jnp.bfloat16),
             jax.ShapeDtypeStruct((OFFSETS, mask_rows, KWIN), jnp.float32),
         ],
-        in_specs=[pl.BlockSpec(memory_space=pltpu.HBM), scalars, scalars, scalars],
-        out_specs=[vmem, vmem],
+        in_specs=[anywhere, scalars, scalars, scalars],
+        out_specs=[anywhere, anywhere],
         scratch_shapes=[
             pltpu.VMEM((OFFSETS, frames, KWIN + LANES), jnp.float32),
+            pltpu.VMEM((OFFSETS, n_det, rows, KWIN), jnp.bfloat16),
+            pltpu.VMEM((OFFSETS, mask_rows, KWIN), jnp.float32),
             dma((OFFSETS,)),
+            dma((OFFSETS + 1,)),
         ],
-        compiler_params=pltpu.CompilerParams(vmem_limit_bytes=16 * 1024 * 1024),
     )(traces, slab_range, table_slot, sample_start)
     return pl.pallas_call(
         functools.partial(kernel, n_slab, n_det),
         out_shape=jax.ShapeDtypeStruct((frames, voxels), jnp.float32),
-        in_specs=[vmem, vmem, anywhere],
+        in_specs=[anywhere, anywhere, anywhere],
         out_specs=vmem,
         scratch_shapes=[
+            pltpu.VMEM((OFFSETS, n_det, rows, KWIN), jnp.bfloat16),
+            pltpu.VMEM((OFFSETS, mask_rows, KWIN), jnp.float32),
             pltpu.VMEM(tables.shape, jnp.bfloat16),
             pltpu.VMEM((n_det, OFFSETS, rows, KWIN), jnp.bfloat16),
             pltpu.VMEM((OFFSETS, mask_rows, KWIN), jnp.float32),
@@ -227,6 +245,8 @@
             pltpu.VMEM((rows, wide), jnp.bfloat16),
             pltpu.VMEM((n_det, rows, wide), jnp.bfloat16),
             dma,
+            dma,
+            dma,
             dma((n_det, OFFSETS)),
             dma((n_det, OFFSETS)),
             dma((OFFSETS,)),
@@ -237,7 +257,7 @@
             dma((n_det,)),
         ],
         compiler_params=pltpu.CompilerParams(
-            collective_id=0, has_side_effects=True, vmem_limit_bytes=16 * 1024 * 1024
+            collective_id=0, has_side_effects=True
         ),
     )(wins, masks, tables)
 

time: 32.2 us -> 31.8 us (0.988)
  local copies, waits for them, and re-layouts: 4.26 us -> 1.67 us
  Pallas kernels: 27.8 us -> 29.9 us
    unnamed x11 -> x1, local copies, waits for them, and re-layouts: 4.26 us -> 1.67 us
    pallas_call x1, Pallas kernels: 2.33 us -> 3.78 us  [body(): pl.pallas_call(functools.partial(cut_kernel, n_slab), out_shape=[jax.Shap...]
    pallas_call x1, Pallas kernels: 25.4 us -> 26.1 us  [body(): pl.pallas_call(functools.partial(kernel, n_slab, n_det), out_shape=jax.Sh...]
where the time goes in v2:
time: 31.8 us; the launch traced here: 31.6 us
  Pallas kernels  29.9 us (94%)
  local copies, waits for them, and re-layouts  1.67 us (5%)
    pallas_call x1, Pallas kernels, body(): pl.pallas_call(functools.partial(kernel, n_slab, n_det), out_shape=jax.Sh...  26.1 us
    pallas_call x1, Pallas kernels, body(): pl.pallas_call(functools.partial(cut_kernel, n_slab), out_shape=[jax.Shap...  3.78 us
    unnamed x1, local copies, waits for them, and re-layouts  1.67 us

profile of v2, /device:TPU:0, one launch (start us, length us, event | category | flops | bytes accessed | tf_op | source)
XLA Modules:
  0.0 31.6 jit_solution(13136794916074021760)
XLA Ops:
  0.0 3.8 %shard_map.55 = (bf16[7,4,32,256]{3,2,1,0:T(8,128)(2,1)}, f32[7,8,256]{2,1,0:T(8,128)}) custom-call(f32[1,128,4096]{2,1,0:T(8,128)} %traces.1, s32[1,2]{1,0:T(1,128)} %slab_range.1, s32[1,7]{1,0:T(1,128)} %table_slot.1, s32[1,7]{1,0:T(1,128)} %sample_start.1), custom_call_target="tpu_custom_call" | custom-call | tf_op jit(solution)/shard_map/pallas_call | solution.py:216
  3.8 26.1 %shard_map.56 = f32[128,512]{1,0:T(8,128)} custom-call(bf16[7,4,32,256]{3,2,1,0:T(8,128)(2,1)} %get-tuple-element.7.wins, f32[7,8,256]{2,1,0:T(8,128)} %get-tuple-element.8.masks, bf16[4,256,512]{2,1,0:T(8,128)(2,1)} %tables.1), custom_call_target="tpu_custom_call" | custom-call | tf_op jit(solution)/shard_map/pallas_call | solution.py:232
  29.9 1.7 %copy.7 = f32[128,512]{1,0:T(8,128)} copy(f32[128,512]{1,0:T(8,128)} %shard_map.56) | data formatting | bytes 524288

commit v3 on v1

--- a/solution.py
+++ b/solution.py
@@ -13,15 +13,16 @@
 RANGE = 3
 LANES = 128
 OFFSETS = 2 * RANGE + 1
-
-
-def cut_kernel(n_slab, traces, slab_range, table_slot, sample_start, wins, masks, spans, sems):
+CUT_LIMIT = 16 * 1024 * 1024
+
+
+def cut_kernel(n_slab, traces, whole, wins, masks, spans, sems):
     slab = lax.axis_index("slab")
     samp, span = traces.shape[2], spans.shape[2]
     n_quarter, _, rows, _ = wins.shape
     loads, inner = [], []
     for o in range(OFFSETS):
-        start = sample_start[0, o]
+        start = whole[0, 2 + OFFSETS + o]
         tile = jnp.minimum(lax.div(start, LANES), (samp - span) // LANES)
         inner.append(start - tile * LANES)
         first = pl.multiple_of(tile * LANES, LANES)
@@ -32,8 +33,8 @@
     mask_rows = lax.broadcasted_iota(jnp.int32, masks.shape[1:], 0)
     for o in range(OFFSETS):
         target = slab + (o - RANGE)
-        active = (slab_range[0, 0] <= target) & (target <= slab_range[0, 1])
-        slot = jnp.where(active, table_slot[0, o], -1)
+        active = (whole[0, 0] <= target) & (target <= whole[0, 1])
+        slot = jnp.where(active, whole[0, 2 + o], -1)
         masks[o] = (mask_rows == slot).astype(jnp.float32)
     far = lax.broadcasted_iota(jnp.int32, (span, KWIN), 0)
     far = far - lax.broadcasted_iota(jnp.int32, (span, KWIN), 1)
@@ -148,7 +149,8 @@
                 win, mask = got_win[c, o], got_mask
             win = win.astype(jnp.float32)
             for t in range(NTAB):
-                bins[t] = bins[t] + mask[o, t : t + 1] * win
+                weight = jnp.concatenate([mask[o, t : t + 1]] * (KWIN // LANES), axis=1)
+                bins[t] = bins[t] + weight * win
         for t in range(NTAB):
             part[c, :, t * KWIN : (t + 1) * KWIN] = bins[t].astype(jnp.bfloat16)
         if order[c] != 0:
@@ -203,16 +205,16 @@
         functools.partial(cut_kernel, n_slab),
         out_shape=[
             jax.ShapeDtypeStruct((n_det, OFFSETS, rows, KWIN), jnp.bfloat16),
-            jax.ShapeDtypeStruct((OFFSETS, mask_rows, KWIN), jnp.float32),
+            jax.ShapeDtypeStruct((OFFSETS, mask_rows, LANES), jnp.float32),
         ],
-        in_specs=[pl.BlockSpec(memory_space=pltpu.HBM), scalars, scalars, scalars],
+        in_specs=[pl.BlockSpec(memory_space=pltpu.HBM), scalars],
         out_specs=[vmem, vmem],
         scratch_shapes=[
             pltpu.VMEM((OFFSETS, frames, KWIN + LANES), jnp.float32),
             dma((OFFSETS,)),
         ],
-        compiler_params=pltpu.CompilerParams(vmem_limit_bytes=16 * 1024 * 1024),
-    )(traces, slab_range, table_slot, sample_start)
+        compiler_params=pltpu.CompilerParams(vmem_limit_bytes=CUT_LIMIT),
+    )(traces, jnp.concatenate([slab_range, table_slot, sample_start], axis=1))
     return pl.pallas_call(
         functools.partial(kernel, n_slab, n_det),
         out_shape=jax.ShapeDtypeStruct((frames, voxels), jnp.float32),
@@ -221,7 +223,7 @@
         scratch_shapes=[
             pltpu.VMEM(tables.shape, jnp.bfloat16),
             pltpu.VMEM((n_det, OFFSETS, rows, KWIN), jnp.bfloat16),
-            pltpu.VMEM((OFFSETS, mask_rows, KWIN), jnp.float32),
+            pltpu.VMEM((OFFSETS, mask_rows, LANES), jnp.float32),
             pltpu.VMEM((n_det, rows, wide), jnp.bfloat16),
             pltpu.VMEM((n_det, rows, wide), jnp.bfloat16),
             pltpu.VMEM((rows, wide), jnp.bfloat16),

time: 32.2 us -> 30.8 us (0.957)
  local copies, waits for them, and re-layouts: 4.26 us -> 2.3 us
  other arithmetic: 0 us -> 0.76 us
    unnamed x11 -> x5, local copies, waits for them, and re-layouts: 4.26 us -> 2.3 us
    concatenate x0 -> x1, other arithmetic: none -> 0.76 us  [body(): jnp.concatenate([slab_range, table_slot, sample_start], axis=1)]
where the time goes in v3:
time: 30.8 us; the launch traced here: 30.7 us
  Pallas kernels  27.6 us (90%)
  local copies, waits for them, and re-layouts  2.3 us (7%)
  other arithmetic  0.76 us (2%)
    pallas_call x1, Pallas kernels, body(): pl.pallas_call(functools.partial(kernel, n_slab, n_det), out_shape=jax.Sh...  25.2 us
    pallas_call x1, Pallas kernels, body(): pl.pallas_call(functools.partial(cut_kernel, n_slab), out_shape=[jax.Shap...  2.32 us
    unnamed x5, local copies, waits for them, and re-layouts  2.3 us
    concatenate x1, other arithmetic, body(): jnp.concatenate([slab_range, table_slot, sample_start], axis=1)  0.76 us

profile of v3, /device:TPU:0, one launch (start us, length us, event | category | flops | bytes accessed | tf_op | source)
XLA Modules:
  0.0 30.7 jit_solution(18162639300528524921)
XLA Ops:
  0.0 0.8 %pad_add_fusion.whole = s32[1,16]{1,0:T(1,128)S(1)} fusion(s32[1,7]{1,0:T(1,128)} %param.9, s32[1,7]{1,0:T(1,128)} %param.8, s32[1,2]{1,0:T(1,128)} %param.7), kind=kLoop, calls=%fused_computation | loop fusion | flops 32 | bytes 128 | tf_op jit(solution)/shard_map/concatenate | solution.py:217
  0.8 0.0 copy-start
  0.8 1.6 %copy-done = f32[1,128,4096]{2,1,0:T(8,128)S(1)} copy-done((f32[1,128,4096]{2,1,0:T(8,128)S(1)}, f32[1,128,4096]{2,1,0:T(8,128)}, u32[]{:S(2)}) %copy-start) | copy-done | bytes 2097176
  2.4 0.0 copy-start.1
  2.4 2.3 %shard_map.55 = (bf16[4,7,32,256]{3,2,1,0:T(8,128)(2,1)S(1)}, f32[7,8,128]{2,1,0:T(8,128)S(1)}) custom-call(f32[1,128,4096]{2,1,0:T(8,128)S(1)} %copy-done, s32[1,16]{1,0:T(1,128)S(1)} %pad_add_fusion.whole), custom_call_target="tpu_custom_call" | custom-call | tf_op jit(solution)/shard_map/pallas_call | solution.py:204
  4.7 0.0 copy-done.1
  4.7 25.2 %shard_map.56 = f32[128,512]{1,0:T(8,128)S(1)} custom-call(bf16[4,7,32,256]{3,2,1,0:T(8,128)(2,1)S(1)} %get-tuple-element.7.send_win, f32[7,8,128]{2,1,0:T(8,128)S(1)} %get-tuple-element.8.send_mask, bf16[4,256,512]{2,1,0:T(8,128)(2,1)S(1)} %copy-done.1), custom_call_target="tpu_custom_call" | custom-call | tf_op jit(solution)/shard_map/pallas_call | solution.py:218
  29.9 0.7 %copy.7 = f32[128,512]{1,0:T(8,128)} copy(f32[128,512]{1,0:T(8,128)S(1)} %shard_map.56) | data formatting | bytes 524288
Async XLA Ops:
  0.8 1.6 %copy-start = (f32[1,128,4096]{2,1,0:T(8,128)S(1)}, f32[1,128,4096]{2,1,0:T(8,128)}, u32[]{:S(2)}) copy-start(f32[1,128,4096]{2,1,0:T(8,128)} %traces.1) | copy-start | bytes 6291460
  2.4 2.3 %copy-start.1 = (bf16[4,256,512]{2,1,0:T(8,128)(2,1)S(1)}, bf16[4,256,512]{2,1,0:T(8,128)(2,1)}, u32[]{:S(2)}) copy-start(bf16[4,256,512]{2,1,0:T(8,128)(2,1)} %tables.1) | copy-start | bytes 3145732
